TPU v7x, 256 devices: a whole 4x4x8 slice. The times are simulated.
256 devices in a mesh: dp: 128 (over y, z, x), mp: 2 (over core).
Axes of the slice: x: 4, y: 4, z: 8, core: 2. Of those that a mesh axis runs over, the one named last changes fastest.
Arguments:
- grad: bfloat16 [32, 1024, 8192], P(None, 'dp', 'mp'), may hold values from -6 to 6
- second_moment: float32 [32, 1024, 8192], P(None, 'dp', 'mp'), may hold values from 0.004 to 20, as said below
- left_root: bfloat16 [2, 128, 1024, 1024], P('mp', 'dp'), as said below
- right_root: bfloat16 [2, 128, 1024, 1024], P('mp', 'dp'), as said below
- owner_slot: int32 [2, 32, 4], replicated, may hold values from 0 to 127, as said below
Outputs:
- update: bfloat16 [32, 1024, 8192], P(None, 'dp', 'mp')
Inputs may be any that keep to these rules, and one draw needn't show every extreme that they name: For each h, owner_slot[h] lists every dp index exactly once: each dp index owns one block of each h. `second_moment`: positive. `left_root`: each square is symmetric positive definite. `right_root`: each square is symmetric positive definite.
All inputs are finite; a program needn't handle non-finite values.
Results may differ from a plain program's by a relative error of at most 0.0049.
Values may be sent and summed in bfloat16 or wider, within the bound.
No kernel may reach another device: no remote copies, remote signals or barrier semaphores. Data moves between devices by JAX's collectives and lax.ppermute only.
A program may use at most 64 MiB of HBM per device.

v0:
```python
import jax
import jax.numpy as jnp
from jax import lax
from jax.sharding import Mesh
from jax.sharding import PartitionSpec as P

DP = ("dp_0", "dp_1", "dp_2")
BETA_TWO = 0.99
ADAM_EPS = 1e-08
NORM_EPS = 1e-06


def one_axis_at_a_time(value, axes):
    for axis in axes:
        value = lax.psum(value, axis)
    return value


def per_device(grad, second_moment, left_root, right_root, owner_slot):
    row_blocks, block_rows, half_cols = grad.shape
    block_size = left_root.shape[-1]
    col_blocks = half_cols // block_size
    dp_count = lax.axis_size(DP)
    mp_index = lax.axis_index("mp")
    owner_index = lax.axis_index(DP)
    widened = grad.astype(jnp.float32)
    moment_new = BETA_TWO * second_moment + (1.0 - BETA_TWO) * widened * widened
    direction = widened / (jnp.sqrt(moment_new) + ADAM_EPS)
    partial_value = jnp.sum(
        (direction * direction).reshape(row_blocks, block_rows, col_blocks, block_size), axis=(1, 3)
    )
    table = lax.dynamic_index_in_dim(owner_slot, mp_index, 0, keepdims=False)
    owner_ids = lax.iota(jnp.int32, dp_count)
    matches = table[None, :, :] == owner_ids[:, None, None]
    select_half = matches.astype(jnp.bfloat16)
    select_full = matches.astype(jnp.float32).reshape(dp_count, row_blocks * col_blocks)
    tiles = grad.reshape(row_blocks, block_rows, col_blocks, block_size)
    outgoing = jnp.einsum("src,rwck->swk", select_half, tiles, preferred_element_type=jnp.float32)
    outgoing = outgoing.astype(jnp.bfloat16).reshape(dp_count, 1, block_rows, block_size)
    totals = one_axis_at_a_time(partial_value, DP)
    own_row = lax.dynamic_index_in_dim(select_full, owner_index, 0, keepdims=False)
    adam_sq = jnp.sum(own_row * totals.reshape(-1))
    left = left_root[0, 0]
    right = right_root[0, 0]
    rows_in = lax.all_to_all(outgoing, DP, split_axis=0, concat_axis=1, tiled=True)
    flat = rows_in.reshape(-1, block_size)
    product = jnp.dot(flat, right, preferred_element_type=jnp.float32).astype(jnp.bfloat16)
    mixed_rows = product.reshape(rows_in.shape)
    mixed = mixed_rows.reshape(block_size, block_size)
    shaped = jnp.dot(left, mixed, preferred_element_type=jnp.float32)
    shaped_sq = jnp.sum(shaped * shaped)
    factor = jnp.sqrt((adam_sq + NORM_EPS) / (shaped_sq + NORM_EPS))
    result = (shaped * factor).astype(jnp.bfloat16).reshape(1, dp_count, block_rows, block_size)
    back = lax.all_to_all(result, DP, split_axis=1, concat_axis=0, tiled=True)
    placed = jnp.einsum(
        "src,swk->rwck",
        select_half,
        back.reshape(dp_count, block_rows, block_size),
        preferred_element_type=jnp.float32,
    )
    return placed.astype(jnp.bfloat16).reshape(row_blocks, block_rows, half_cols)


def solution(mesh):
    split = Mesh(mesh.devices.reshape(4, 8, 4, mesh.shape["mp"]), ("dp_0", "dp_1", "dp_2", "mp"))
    return jax.shard_map(
        per_device,
        mesh=split,
        in_specs=(
            P(None, DP, "mp"),
            P(None, DP, "mp"),
            P("mp", DP, None, None),
            P("mp", DP, None, None),
            P(),
        ),
        out_specs=P(None, DP, "mp"),
        check_vma=False,
    )
```

profile of v0, /device:TPU:32, one launch (start us, length us, event | category | flops | bytes accessed | tf_op | source)
XLA Modules:
  0.0 170.4 jit_solution(4554805656612453106)
XLA Ops:
  0.0 0.0 copy-start
  0.0 0.8 fusion.41
  0.8 4.4 %fusion.18 = bf16[128,1,8,1024]{3,0,2,1:T(8,128)(2,1)S(1)} fusion(bf16[32,8,4,1024]{3,1,2,0:T(8,128)(2,1)} %bitcast.59, s32[32,4]{0,1:T(4,128)S(1)} %fusion.41), kind=kOutput, calls=%fused_computation.22 | convolution fusion | flops 269500416 | bytes 4194816 | tf_op jit(solution)/shard_map/src,rwck->swk/dot_general | solution.py:38
  5.2 2.5 %copy.28 = bf16[128,1,8,1024]{3,2,1,0:T(8,128)(2,1)} copy(bf16[128,1,8,1024]{3,0,2,1:T(8,128)(2,1)S(1)} %fusion.18) | data formatting | bytes 4194304 | tf_op jit(solution)/shard_map/reshape | solution.py:39
  7.7 0.0 copy-start.1
  7.7 15.6 %all-to-all-start = ((bf16[128,1,8,1024]{3,2,1,0:T(8,128)(2,1)}), bf16[128,1,8,1024]{3,2,1,0:T(8,128)(2,1)}, u32[]{:S(2)}, u32[]{:S(2)}) async-start(bf16[128,1,8,1024]{3,2,1,0:T(8,128)(2,1)} %copy.28), calls=%async_computation | async-start | bytes 4194304 | tf_op jit(solution)/shard_map/all_to_all | solution.py:45
  23.3 0.0 copy-done.1
  23.3 0.1 copy.29
  23.4 0.1 eq.28
  23.5 6.0 %fusion.4 = f32[32,4096]{1,0:T(8,128)S(1)} fusion(f32[32,8,4096]{2,1,0:T(8,128)} %param.6, bf16[32,8,4096]{2,1,0:T(8,128)(2,1)} %param.5), kind=kLoop, calls=%fused_computation.9 | loop fusion | flops 9306112 | bytes 6815744 | tf_op jit(solution)/shard_map/reduce_sum | solution.py:29
  29.5 0.4 reduce_sum.35
  29.9 0.1 reduce_sum.36
  30.0 0.1 copy.37
  30.1 11.2 %psum.21 = f32[32,4]{0,1:T(4,128)S(1)} all-reduce(f32[32,4]{0,1:T(4,128)S(1)} %copy.37), channel_id=1, replica_groups=mesh['dp_0'=4,'dp_1'=8,'dp_2'=4,'mp'=2] {'dp_0'}, use_global_device_ids=true, to_apply=%region_2.3 | all-reduce | flops 128 | bytes 1024 | tf_op jit(solution)/shard_map/psum | solution.py:15
  41.3 36.2 %psum.22 = f32[32,4]{0,1:T(4,128)S(1)} all-reduce(f32[32,4]{0,1:T(4,128)S(1)} %psum.21), channel_id=1, replica_groups=mesh['dp_0'=4,'dp_1'=8,'dp_2'=4,'mp'=2] {'dp_1'}, use_global_device_ids=true, to_apply=%region_3.4 | all-reduce | flops 128 | bytes 1024 | tf_op jit(solution)/shard_map/psum | solution.py:15
  77.5 0.1 copy.31
  77.6 0.1 reshape.37
  77.7 10.8 %psum.23 = f32[128]{0:T(128)S(1)} all-reduce(f32[128]{0:T(128)S(1)} %reshape.37), channel_id=1, replica_groups=mesh['dp_0'=4,'dp_1'=8,'dp_2'=4,'mp'=2] {'dp_2'}, use_global_device_ids=true, to_apply=%region_4.5 | all-reduce | flops 128 | bytes 1024 | tf_op jit(solution)/shard_map/psum | solution.py:15
  88.5 0.7 fusion.36
  89.9 0.0 all-to-all-done
  89.9 0.0 copy-done
  89.9 9.2 %multiply_reduce_fusion = (f32[]{:T(128)}, f32[1024,1024]{0,1:T(8,128)}) fusion(bf16[1,1,1024,1024]{3,2,1,0:T(8,128)(2,1)S(1)} %copy-done, bf16[128,1,8,1024]{3,2,1,0:T(8,128)(2,1)} %all-to-all-done, bf16[1,1,1024,1024]{3,2,1,0:T(8,128)(2,1)} %param.7), kind=kOutput, calls=%fused_computation.8 | convolution fusion | flops 4298113024 | bytes 10485764 | tf_op jit(solution)/shard_map/dot_general | solution.py:50
  99.9 2.8 %fusion.5 = bf16[1,128,8,1024]{3,2,0,1:T(8,128)(2,1)S(1)} fusion(f32[1024,1024]{0,1:T(8,128)} %get-tuple-element.6, f32[]{:T(128)S(6)} %sqrt.7), kind=kLoop, calls=%fused_computation.10 | loop fusion | flops 2097152 | bytes 6291460 | tf_op jit(solution)/shard_map/reshape | solution.py:53
  102.6 58.6 %all_to_all.8 = bf16[1,128,8,1024]{3,2,0,1:T(8,128)(2,1)S(1)} all-to-all(bf16[1,128,8,1024]{3,2,0,1:T(8,128)(2,1)S(1)} %fusion.5), channel_id=1, replica_groups=mesh['dp_0'=4,'dp_1'=8,'dp_2'=4,'mp'=2] {'dp_0','dp_1','dp_2'}, dimensions={1} | all-to-all | bytes 4194304 | tf_op jit(solution)/shard_map/all_to_all | solution.py:54
  161.2 1.7 %convert_bitcast_fusion = bf16[32,8,4,1024]{3,0,2,1:T(8,128)(2,1)S(1)} fusion(bf16[1,128,8,1024]{3,2,0,1:T(8,128)(2,1)S(1)} %all_to_all.8, s32[32,4]{0,1:T(4,128)S(1)} %fusion.41), kind=kOutput, calls=%fused_computation.20 | convolution fusion | flops 269500416 | bytes 4194816 | tf_op jit(solution)/shard_map/src,swk->rwck/dot_general | solution.py:55
  163.0 3.0 %copy.34 = bf16[32,8,4,1024]{3,2,1,0:T(4,128)(2,1)} copy(bf16[32,8,4,1024]{3,0,2,1:T(8,128)(2,1)S(1)} %convert_bitcast_fusion) | data formatting | bytes 4194304 | tf_op jit(solution)/shard_map/convert_element_type | solution.py:61
  165.9 4.5 %reshape.40 = bf16[32,8,4096]{2,1,0:T(8,128)(2,1)} reshape(bf16[32,8,4,1024]{3,2,1,0:T(4,128)(2,1)} %copy.34) | data formatting | bytes 4194304 | tf_op jit(solution)/shard_map/reshape | solution.py:61
  (1 shorter events, 0.0 us)
Async XLA Ops:
  0.0 89.9 %copy-start = (bf16[1,1,1024,1024]{3,2,1,0:T(8,128)(2,1)S(1)}, bf16[1,1,1024,1024]{3,2,1,0:T(8,128)(2,1)}, u32[]{:S(2)}) copy-start(bf16[1,1,1024,1024]{3,2,1,0:T(8,128)(2,1)} %param.8) | copy-start | bytes 6291460
  7.7 15.6 %copy-start.1 = (s32[2,32,4]{1,2,0:T(4,128)S(1)}, s32[2,32,4]{1,2,0:T(4,128)}, u32[]{:S(2)}) copy-start(s32[2,32,4]{1,2,0:T(4,128)} %param.9) | copy-start | bytes 3076
  7.7 82.2 %all-to-all-start = ((bf16[128,1,8,1024]{3,2,1,0:T(8,128)(2,1)}), bf16[128,1,8,1024]{3,2,1,0:T(8,128)(2,1)}, u32[]{:S(2)}, u32[]{:S(2)}) async-start(bf16[128,1,8,1024]{3,2,1,0:T(8,128)(2,1)} %copy.28), calls=%async_computation | async-start | bytes 4194304 | tf_op jit(solution)/shard_map/all_to_all | solution.py:45
where the time goes:
time: 171 us; the launch traced here: 170 us
  blocking collectives  117 us (68%)
  starting transfers between devices  15.6 us (9%)
  matrix products  15.3 us (9%)
  local copies, waits for them, and re-layouts  11.6 us (7%)
  other arithmetic  9.62 us (6%)
    all_to_all x1, blocking collectives, per_device(): back = lax.all_to_all(result, DP, split_axis=1, concat_axis=0, tiled=True)  58.6 us
    psum x3, blocking collectives, one_axis_at_a_time(): value = lax.psum(value, axis)  58.2 us
    all_to_all x1, starting transfers between devices, per_device(): lax.all_to_all(outgoing, DP, split_axis=0, concat_axis=1, tiled=True)  15.6 us
    dot_general x1, matrix products, per_device(): shaped = jnp.dot(left, mixed, preferred_element_type=jnp.float32)  9.24 us
    reduce_sum x2, other arithmetic, per_device(): jnp.sum((direction * direction).reshape(row_blocks, block_rows, col_block...  6.16 us
    reshape x1, local copies, waits for them, and re-layouts, per_device(): placed.astype(jnp.bfloat16).reshape(row_blocks, block_rows, half_cols)  4.45 us
    dot_general x1, matrix products, per_device(): jnp.einsum('src,rwck->swk', select_half, tiles, preferred_element_type=jn...  4.35 us
  transfers between devices with their start and end apart: 1, of which 0 were waited for; matrix products, arithmetic and copies ran while one was open for 5% of the time, Pallas kernels for 0%

commit v1 on v0

--- a/solution.py
+++ b/solution.py
@@ -51,7 +51,9 @@
     shaped_sq = jnp.sum(shaped * shaped)
     factor = jnp.sqrt((adam_sq + NORM_EPS) / (shaped_sq + NORM_EPS))
     result = (shaped * factor).astype(jnp.bfloat16).reshape(1, dp_count, block_rows, block_size)
-    back = lax.all_to_all(result, DP, split_axis=1, concat_axis=0, tiled=True)
+    back = jnp.concatenate(
+        lax.all_to_all(jnp.stack(jnp.split(result, lax.axis_size(DP), axis=1)), DP, 0, 0), axis=0
+    )
     placed = jnp.einsum(
         "src,swk->rwck",
         select_half,

time: 171 us -> 182 us (1.064)
  blocking collectives: 117 us -> 126 us
    psum x3, blocking collectives: 58.2 us -> 70.8 us  [one_axis_at_a_time(): value = lax.psum(value, axis)]
    all_to_all x1, blocking collectives: 58.6 us -> 55.4 us  [per_device(): lax.all_to_all(jnp.stack(jnp.split(result, lax.axis_size(DP), axis=1)), D...]
  transfers between devices with their start and end apart: 1 -> 1, of which waited for: 0 -> 0; matrix products, arithmetic and copies ran while one was open for 5% -> 4% of each run, Pallas kernels for 0% -> 0%
where the time goes in v1:
time: 182 us; the launch traced here: 181 us
  blocking collectives  126 us (69%)
  starting transfers between devices  15.6 us (9%)
  matrix products  15.3 us (8%)
  local copies, waits for them, and re-layouts  11.9 us (7%)
  other arithmetic  9.62 us (5%)
  between operations  2.54 us (1%)
    psum x3, blocking collectives, one_axis_at_a_time(): value = lax.psum(value, axis)  70.8 us
    all_to_all x1, blocking collectives, per_device(): lax.all_to_all(jnp.stack(jnp.split(result, lax.axis_size(DP), axis=1)), D...  55.4 us
    all_to_all x1, starting transfers between devices, per_device(): lax.all_to_all(outgoing, DP, split_axis=0, concat_axis=1, tiled=True)  15.6 us
    dot_general x1, matrix products, per_device(): shaped = jnp.dot(left, mixed, preferred_element_type=jnp.float32)  9.24 us
    reduce_sum x2, other arithmetic, per_device(): jnp.sum((direction * direction).reshape(row_blocks, block_rows, col_block...  6.16 us
    reshape x1, local copies, waits for them, and re-layouts, per_device(): placed.astype(jnp.bfloat16).reshape(row_blocks, block_rows, half_cols)  4.45 us
    dot_general x1, matrix products, per_device(): jnp.einsum('src,rwck->swk', select_half, tiles, preferred_element_type=jn...  4.35 us
  transfers between devices with their start and end apart: 1, of which 0 were waited for; matrix products, arithmetic and copies ran while one was open for 4% of the time, Pallas kernels for 0%

profile of v1, /device:TPU:32, one launch (start us, length us, event | category | flops | bytes accessed | tf_op | source)
XLA Modules:
  0.0 181.1 jit_solution(12323805415066190828)
XLA Ops:
  0.0 0.0 copy-start
  0.0 0.8 fusion.41
  0.8 4.4 %fusion.18 = bf16[128,1,8,1024]{3,0,2,1:T(8,128)(2,1)S(1)} fusion(bf16[32,8,4,1024]{3,1,2,0:T(8,128)(2,1)} %bitcast.570, s32[32,4]{0,1:T(4,128)S(1)} %fusion.41), kind=kOutput, calls=%fused_computation.22 | convolution fusion | flops 269500416 | bytes 4194816 | tf_op jit(solution)/shard_map/src,rwck->swk/dot_general | solution.py:38
  5.2 2.5 %copy.4071 = bf16[128,1,8,1024]{3,2,1,0:T(8,128)(2,1)} copy(bf16[128,1,8,1024]{3,0,2,1:T(8,128)(2,1)S(1)} %fusion.18) | data formatting | bytes 4194304 | tf_op jit(solution)/shard_map/reshape | solution.py:39
  7.7 0.0 copy-start.1
  7.7 15.6 %all-to-all-start = ((bf16[128,1,8,1024]{3,2,1,0:T(8,128)(2,1)}), bf16[128,1,8,1024]{3,2,1,0:T(8,128)(2,1)}, u32[]{:S(2)}, u32[]{:S(2)}) async-start(bf16[128,1,8,1024]{3,2,1,0:T(8,128)(2,1)} %copy.4071), calls=%async_computation | async-start | bytes 4194304 | tf_op jit(solution)/shard_map/all_to_all | solution.py:45
  23.3 0.0 copy-done.1
  23.3 0.1 copy.4072
  23.4 0.1 eq.28
  23.5 6.0 %fusion.4 = f32[32,4096]{1,0:T(8,128)S(1)} fusion(f32[32,8,4096]{2,1,0:T(8,128)} %param.6, bf16[32,8,4096]{2,1,0:T(8,128)(2,1)} %param.5), kind=kLoop, calls=%fused_computation.9 | loop fusion | flops 9306112 | bytes 6815744 | tf_op jit(solution)/shard_map/reduce_sum | solution.py:29
  29.5 0.4 reduce_sum.35
  29.9 0.1 reduce_sum.36
  30.0 17.6 %psum.21 = f32[32,4]{1,0:T(8,128)S(1)} all-reduce(f32[32,4]{1,0:T(8,128)S(1)} %reduce_sum.36), channel_id=1, replica_groups=mesh['dp_0'=4,'dp_1'=8,'dp_2'=4,'mp'=2] {'dp_0'}, use_global_device_ids=true, to_apply=%region_2.3 | all-reduce | flops 128 | bytes 1024 | tf_op jit(solution)/shard_map/psum | solution.py:15
  47.7 42.6 %psum.22 = f32[32,4]{1,0:T(8,128)S(1)} all-reduce(f32[32,4]{1,0:T(8,128)S(1)} %psum.21), channel_id=1, replica_groups=mesh['dp_0'=4,'dp_1'=8,'dp_2'=4,'mp'=2] {'dp_1'}, use_global_device_ids=true, to_apply=%region_3.4 | all-reduce | flops 128 | bytes 1024 | tf_op jit(solution)/shard_map/psum | solution.py:15
  90.2 0.1 reshape.30
  90.3 10.6 %psum.23 = f32[128]{0:T(128)S(1)} all-reduce(f32[128]{0:T(128)S(1)} %reshape.30), channel_id=1, replica_groups=mesh['dp_0'=4,'dp_1'=8,'dp_2'=4,'mp'=2] {'dp_2'}, use_global_device_ids=true, to_apply=%region_4.5 | all-reduce | flops 128 | bytes 1024 | tf_op jit(solution)/shard_map/psum | solution.py:15
  100.9 0.7 fusion.36
  102.3 0.0 all-to-all-done
  102.3 0.0 copy-done
  102.3 9.2 %multiply_reduce_fusion = (f32[]{:T(128)}, f32[1024,1024]{0,1:T(8,128)}) fusion(bf16[1,1,1024,1024]{3,2,1,0:T(8,128)(2,1)S(1)} %copy-done, bf16[128,1,8,1024]{3,2,1,0:T(8,128)(2,1)} %all-to-all-done, bf16[1,1,1024,1024]{3,2,1,0:T(8,128)(2,1)} %param.7), kind=kOutput, calls=%fused_computation.8 | convolution fusion | flops 4298113024 | bytes 10485764 | tf_op jit(solution)/shard_map/dot_general | solution.py:50
  112.3 2.8 %fusion.5 = bf16[1,128,8,1024]{3,2,1,0:T(8,128)(2,1)S(1)} fusion(f32[1024,1024]{0,1:T(8,128)} %get-tuple-element.6, f32[]{:T(128)S(6)} %sqrt.7), kind=kLoop, calls=%fused_computation.10 | loop fusion | flops 2097152 | bytes 6291460 | tf_op jit(solution)/shard_map/reshape | solution.py:53
  116.6 55.4 %all_to_all.14 = bf16[128,1,1,8,1024]{4,3,2,1,0:T(8,128)(2,1)S(1)} all-to-all(bf16[128,1,1,8,1024]{4,3,2,1,0:T(8,128)(2,1)S(1)} %constant_dynamic-update-slice_fusion), channel_id=1, replica_groups=mesh['dp_0'=4,'dp_1'=8,'dp_2'=4,'mp'=2] {'dp_0','dp_1','dp_2'}, dimensions={0} | all-to-all | bytes 4194304 | tf_op jit(solution)/shard_map/all_to_all | solution.py:55
  171.9 1.7 convert_bitcast_fusion
  173.6 3.0 %copy.4074 = bf16[32,8,4,1024]{3,2,1,0:T(4,128)(2,1)} copy(bf16[32,8,4,1024]{3,0,2,1:T(8,128)(2,1)S(1)} %convert_bitcast_fusion) | data formatting | bytes 4194304 | tf_op jit(solution)/shard_map/convert_element_type | solution.py:63
  176.6 4.5 %reshape.32 = bf16[32,8,4096]{2,1,0:T(8,128)(2,1)} reshape(bf16[32,8,4,1024]{3,2,1,0:T(4,128)(2,1)} %copy.4074) | data formatting | bytes 4194304 | tf_op jit(solution)/shard_map/reshape | solution.py:63
  (129 shorter events, 0.5 us)
Async XLA Ops:
  0.0 102.3 %copy-start = (bf16[1,1,1024,1024]{3,2,1,0:T(8,128)(2,1)S(1)}, bf16[1,1,1024,1024]{3,2,1,0:T(8,128)(2,1)}, u32[]{:S(2)}) copy-start(bf16[1,1,1024,1024]{3,2,1,0:T(8,128)(2,1)} %param.8) | copy-start | bytes 6291460
  7.7 15.6 %copy-start.1 = (s32[2,32,4]{1,2,0:T(4,128)S(1)}, s32[2,32,4]{1,2,0:T(4,128)}, u32[]{:S(2)}) copy-start(s32[2,32,4]{1,2,0:T(4,128)} %param.9) | copy-start | bytes 3076
  7.7 94.6 %all-to-all-start = ((bf16[128,1,8,1024]{3,2,1,0:T(8,128)(2,1)}), bf16[128,1,8,1024]{3,2,1,0:T(8,128)(2,1)}, u32[]{:S(2)}, u32[]{:S(2)}) async-start(bf16[128,1,8,1024]{3,2,1,0:T(8,128)(2,1)} %copy.4071), calls=%async_computation | async-start | bytes 4194304 | tf_op jit(solution)/shard_map/all_to_all | solution.py:45

commit v2 on v0

--- a/solution.py
+++ b/solution.py
@@ -12,7 +12,7 @@
 
 def one_axis_at_a_time(value, axes):
     for axis in axes:
-        value = lax.psum(value, axis)
+        value = jnp.sum(lax.all_gather(value, axis), axis=0)
     return value
 
 

time: 171 us -> 176 us (1.029)
  blocking collectives: 117 us -> 122 us
    all_gather x0 -> x3, blocking collectives: none -> 67.4 us  [one_axis_at_a_time(): value = jnp.sum(lax.all_gather(value, axis), axis=0)]
    psum x3 -> x0, blocking collectives: 58.2 us -> none  [one_axis_at_a_time(): value = lax.psum(value, axis)]
    all_to_all x1, blocking collectives: 58.6 us -> 54.7 us  [per_device(): back = lax.all_to_all(result, DP, split_axis=1, concat_axis=0, tiled=True)]
  transfers between devices with their start and end apart: 1 -> 1, of which waited for: 0 -> 0; matrix products, arithmetic and copies ran while one was open for 5% -> 4% of each run, Pallas kernels for 0% -> 0%
where the time goes in v2:
time: 176 us
  blocking collectives  122 us (69%)
  starting transfers between devices  15.6 us (9%)
  matrix products  15.3 us (9%)
  local copies, waits for them, and re-layouts  11.6 us (7%)
  other arithmetic  9.67 us (5%)
    all_gather x3, blocking collectives, one_axis_at_a_time(): value = jnp.sum(lax.all_gather(value, axis), axis=0)  67.4 us
    all_to_all x1, blocking collectives, per_device(): back = lax.all_to_all(result, DP, split_axis=1, concat_axis=0, tiled=True)  54.7 us
    all_to_all x1, starting transfers between devices, per_device(): lax.all_to_all(outgoing, DP, split_axis=0, concat_axis=1, tiled=True)  15.6 us
    dot_general x1, matrix products, per_device(): shaped = jnp.dot(left, mixed, preferred_element_type=jnp.float32)  9.25 us
    reduce_sum x2, other arithmetic, per_device(): jnp.sum((direction * direction).reshape(row_blocks, block_rows, col_block...  6.16 us
    reshape x1, local copies, waits for them, and re-layouts, per_device(): placed.astype(jnp.bfloat16).reshape(row_blocks, block_rows, half_cols)  4.45 us
    dot_general x1, matrix products, per_device(): jnp.einsum('src,rwck->swk', select_half, tiles, preferred_element_type=jn...  4.35 us
  transfers between devices with their start and end apart: 1, of which 0 were waited for; matrix products, arithmetic and copies ran while one was open for 4% of the time, Pallas kernels for 0%

profile of v2, /device:TPU:32, one launch (start us, length us, event | category | flops | bytes accessed | tf_op | source)
XLA Modules:
  0.0 175.8 jit_solution(18205387848069560403)
XLA Ops:
  0.0 0.0 copy-start
  0.0 0.8 fusion.41
  0.8 4.4 %fusion.18 = bf16[128,1,8,1024]{3,0,2,1:T(8,128)(2,1)S(1)} fusion(bf16[32,8,4,1024]{3,1,2,0:T(8,128)(2,1)} %bitcast.62, s32[32,4]{0,1:T(4,128)S(1)} %fusion.41), kind=kOutput, calls=%fused_computation.22 | convolution fusion | flops 269500416 | bytes 4194816 | tf_op jit(solution)/shard_map/src,rwck->swk/dot_general | solution.py:38
  5.2 2.5 %copy.29 = bf16[128,1,8,1024]{3,2,1,0:T(8,128)(2,1)} copy(bf16[128,1,8,1024]{3,0,2,1:T(8,128)(2,1)S(1)} %fusion.18) | data formatting | bytes 4194304 | tf_op jit(solution)/shard_map/reshape | solution.py:39
  7.7 0.0 copy-start.1
  7.7 15.6 %all-to-all-start = ((bf16[128,1,8,1024]{3,2,1,0:T(8,128)(2,1)}), bf16[128,1,8,1024]{3,2,1,0:T(8,128)(2,1)}, u32[]{:S(2)}, u32[]{:S(2)}) async-start(bf16[128,1,8,1024]{3,2,1,0:T(8,128)(2,1)} %copy.29), calls=%async_computation | async-start | bytes 4194304 | tf_op jit(solution)/shard_map/all_to_all | solution.py:45
  23.3 0.0 copy-done.1
  23.3 0.1 copy.30
  23.4 0.1 eq.28
  23.5 6.0 %fusion.4 = f32[32,4096]{1,0:T(8,128)S(1)} fusion(f32[32,8,4096]{2,1,0:T(8,128)} %param.6, bf16[32,8,4096]{2,1,0:T(8,128)(2,1)} %param.5), kind=kLoop, calls=%fused_computation.9 | loop fusion | flops 9306112 | bytes 6815744 | tf_op jit(solution)/shard_map/reduce_sum | solution.py:29
  29.5 0.4 reduce_sum.62
  29.9 0.1 reduce_sum.63
  30.0 0.1 copy.38
  30.1 11.5 %all-gather.3 = f32[4,32,4]{1,2,0:T(4,128)S(1)} all-gather(f32[1,32,4]{1,2,0:T(4,128)S(1)} %bitcast.63), channel_id=2, replica_groups=mesh['dp_0'=4,'dp_1'=8,'dp_2'=4,'mp'=2] {'dp_0'}, dimensions={0}, use_global_device_ids=true | all-gather | bytes 2560 | tf_op jit(solution)/shard_map/all_gather | solution.py:15
  41.6 44.7 %all-gather.4 = f32[8,32,4]{1,2,0:T(4,128)S(1)} all-gather(f32[1,32,4]{1,2,0:T(4,128)S(1)} %bitcast.65), channel_id=3, replica_groups=mesh['dp_0'=4,'dp_1'=8,'dp_2'=4,'mp'=2] {'dp_1'}, dimensions={0}, use_global_device_ids=true | all-gather | bytes 4608 | tf_op jit(solution)/shard_map/all_gather | solution.py:15
  86.3 11.3 %all-gather.5 = f32[4,32,4]{1,2,0:T(4,128)S(1)} all-gather(f32[1,32,4]{1,2,0:T(4,128)S(1)} %bitcast.64), channel_id=4, replica_groups=mesh['dp_0'=4,'dp_1'=8,'dp_2'=4,'mp'=2] {'dp_2'}, dimensions={0}, use_global_device_ids=true | all-gather | bytes 2560 | tf_op jit(solution)/shard_map/all_gather | solution.py:15
  97.6 0.1 copy.32
  97.6 0.1 reshape.37
  97.8 0.7 fusion.36
  99.1 0.0 all-to-all-done
  99.1 0.0 copy-done
  99.2 9.2 %multiply_reduce_fusion = (f32[]{:T(128)}, f32[1024,1024]{0,1:T(8,128)}) fusion(bf16[1,1,1024,1024]{3,2,1,0:T(8,128)(2,1)S(1)} %copy-done, bf16[128,1,8,1024]{3,2,1,0:T(8,128)(2,1)} %all-to-all-done, bf16[1,1,1024,1024]{3,2,1,0:T(8,128)(2,1)} %param.7), kind=kOutput, calls=%fused_computation.8 | convolution fusion | flops 4298113024 | bytes 10485764 | tf_op jit(solution)/shard_map/dot_general | solution.py:50
  109.1 2.8 %fusion.5 = bf16[1,128,8,1024]{3,2,0,1:T(8,128)(2,1)S(1)} fusion(f32[1024,1024]{0,1:T(8,128)} %get-tuple-element.6, f32[]{:T(128)S(6)} %sqrt.7), kind=kLoop, calls=%fused_computation.10 | loop fusion | flops 2097152 | bytes 6291460 | tf_op jit(solution)/shard_map/reshape | solution.py:53
  111.9 54.7 %all_to_all.8 = bf16[1,128,8,1024]{3,2,0,1:T(8,128)(2,1)S(1)} all-to-all(bf16[1,128,8,1024]{3,2,0,1:T(8,128)(2,1)S(1)} %fusion.5), channel_id=1, replica_groups=mesh['dp_0'=4,'dp_1'=8,'dp_2'=4,'mp'=2] {'dp_0','dp_1','dp_2'}, dimensions={1} | all-to-all | bytes 4194304 | tf_op jit(solution)/shard_map/all_to_all | solution.py:54
  166.7 1.7 convert_bitcast_fusion
  168.4 3.0 %copy.35 = bf16[32,8,4,1024]{3,2,1,0:T(4,128)(2,1)} copy(bf16[32,8,4,1024]{3,0,2,1:T(8,128)(2,1)S(1)} %convert_bitcast_fusion) | data formatting | bytes 4194304 | tf_op jit(solution)/shard_map/convert_element_type | solution.py:61
  171.4 4.5 %reshape.40 = bf16[32,8,4096]{2,1,0:T(8,128)(2,1)} reshape(bf16[32,8,4,1024]{3,2,1,0:T(4,128)(2,1)} %copy.35) | data formatting | bytes 4194304 | tf_op jit(solution)/shard_map/reshape | solution.py:61
  (4 shorter events, 0.1 us)
Async XLA Ops:
  0.0 99.1 %copy-start = (bf16[1,1,1024,1024]{3,2,1,0:T(8,128)(2,1)S(1)}, bf16[1,1,1024,1024]{3,2,1,0:T(8,128)(2,1)}, u32[]{:S(2)}) copy-start(bf16[1,1,1024,1024]{3,2,1,0:T(8,128)(2,1)} %param.8) | copy-start | bytes 6291460
  7.7 15.6 %copy-start.1 = (s32[2,32,4]{1,2,0:T(4,128)S(1)}, s32[2,32,4]{1,2,0:T(4,128)}, u32[]{:S(2)}) copy-start(s32[2,32,4]{1,2,0:T(4,128)} %param.9) | copy-start | bytes 3076
  7.7 91.5 %all-to-all-start = ((bf16[128,1,8,1024]{3,2,1,0:T(8,128)(2,1)}), bf16[128,1,8,1024]{3,2,1,0:T(8,128)(2,1)}, u32[]{:S(2)}, u32[]{:S(2)}) async-start(bf16[128,1,8,1024]{3,2,1,0:T(8,128)(2,1)} %copy.29), calls=%async_computation | async-start | bytes 4194304 | tf_op jit(solution)/shard_map/all_to_all | solution.py:45
